TPU v7x, 256 devices: a whole 4x4x8 slice. The times are simulated.
256 devices in a mesh: dom: 64 (over x_lo, z, y), orb: 4 (over x_hi, core).
Axes of the slice: x: 4 (x_hi: 2, x_lo: 2; x = x_hi * 2 + x_lo), y: 4, z: 8, core: 2. Of those that a mesh axis runs over, the one named last changes fastest.
Arguments:
- orbitals: bfloat16 [128, 4, 1024, 512], P('dom', None, None, 'orb'), may hold values from -6 to 6
- slot_ids: int32 [128, 4], P('dom'), may hold values from 0 to 15, as said below
- slot_count: int32 [128], P('dom'), may hold values from 1 to 4, as said below
- band_tiles: bfloat16 [16, 3, 512, 512], P(None, None, 'dom', 'orb'), may hold values from -0.15625 to 0.15625
- pattern: int32 [16, 3], replicated, may hold values 0 or 1
- occupation: float32 [16, 512], P(None, 'orb'), may hold values from 0.0005 to 0.005
Outputs:
- rotated: bfloat16 [128, 4, 1024, 512], P('dom', None, None, 'orb')
- density: float32 [128, 1024], P('dom')
Inputs may be any that keep to these rules, and one draw needn't show every extreme that they name: `slot_ids`: each row names 4 consecutive orbital blocks counted modulo 16: slot l holds (s + l) mod 16, where the first block s of a grid block may be any of the 16 blocks. The slots in use on grid block g are its first slot_count[g]; some grid block uses all 4.
All inputs are finite; a program needn't handle non-finite values.
Results may differ from a plain program's by a relative error of at most 0.00094.
Values may be sent and summed in bfloat16 or wider, within the bound.
No kernel may reach another device: no remote copies, remote signals or barrier semaphores. Data moves between devices by JAX's collectives and lax.ppermute only.
A program may use at most 128 MiB of HBM per device.

v0:
```python
import jax
import jax.numpy as jnp
from jax import lax
from jax.sharding import Mesh
from jax.sharding import PartitionSpec as P

DOM = ("dom_0", "dom_1", "dom_2")


def laid_out(tiles, dim):
    shape = list(tiles.shape[1:])
    shape[dim] *= tiles.shape[0]
    return jnp.moveaxis(tiles, 0, dim).reshape(shape)


def all_blocks(x, axes, sequence):
    tiles = x
    for k in sequence:
        tiles = lax.all_gather(tiles, axes[k])
    done = sequence[::-1]
    back = [done.index(k) for k in range(len(axes))]
    tiles = tiles.transpose(*back, *range(len(axes), tiles.ndim))
    return tiles.reshape(-1, *x.shape)


def whole_of(x, axes, sequence, dim):
    return laid_out(all_blocks(x, axes, sequence), dim)


def from_everyone(x, axis):
    peers = lax.axis_size(axis)
    return lax.all_to_all(jnp.broadcast_to(x[None], (peers, *x.shape)), axis, 0, 0, tiled=True)


def of_everyone(x, axis):
    return from_everyone(x, axis).sum(axis=0)


def select_tiles(band_full, pattern, slot_ids, slot_count):
    slots_per = slot_ids.shape[1]
    band_count = pattern.shape[1]
    half_band = (band_count - 1) // 2
    active = jnp.arange(slots_per, dtype=jnp.int32)[None, :] < slot_count[:, None]
    source = slot_ids[:, :, None]
    target = slot_ids[:, None, :]
    offset = target - source + half_band
    inside = (offset >= 0) & (offset < band_count)
    column = jnp.clip(offset, 0, band_count - 1)
    keeping = inside & (pattern[source, column] == 1) & active[:, :, None] & active[:, None, :]
    picked = band_full[source, column]
    return jnp.where(keeping[:, :, :, None, None], picked, jnp.zeros((), picked.dtype))


def rotate(values, tile_set):
    return jnp.einsum("glpi,glmij->gmpj", values, tile_set, preferred_element_type=jnp.float32)


def local(orbitals, slot_ids, slot_count, band_tiles, pattern, occupation):
    all_rows = whole_of(band_tiles, DOM, (0, 1, 2), 2)
    tile_set = select_tiles(all_rows, pattern, slot_ids, slot_count)
    rotated_f = rotate(lax.all_gather(orbitals, "orb", axis=3, tiled=True), tile_set)
    rotated = rotated_f.astype(jnp.bfloat16)
    onehot = (
        slot_ids[:, :, None] == jnp.arange(occupation.shape[0], dtype=jnp.int32)[None, None, :]
    ).astype(jnp.float32)
    weights = jnp.einsum("glb,bj->glj", onehot, occupation, precision=lax.Precision.HIGHEST)
    widened = rotated.astype(jnp.float32)
    square = widened * widened
    partial_density = jnp.einsum("gmpj,gmj->gp", square, weights, precision=lax.Precision.HIGHEST)
    density = of_everyone(partial_density, "orb")
    return (rotated, density)


def solution(mesh):
    torus = Mesh(
        mesh.devices.reshape(2, 8, 4, mesh.shape["orb"]), ("dom_0", "dom_1", "dom_2", "orb")
    )
    return jax.shard_map(
        local,
        mesh=torus,
        in_specs=(
            P(DOM, None, None, "orb"),
            P(DOM, None),
            P(DOM),
            P(None, None, DOM, "orb"),
            P(),
            P(None, "orb"),
        ),
        out_specs=(P(DOM, None, None, "orb"), P(DOM, None)),
        check_vma=False,
    )
```

profile of v0, /device:TPU:1, one launch (start us, length us, event | category | flops | bytes accessed | tf_op | source)
XLA Modules:
  0.0 223.0 jit_solution(2459626745871815533)
XLA Ops:
  7.2 0.0 copy-start
  7.2 0.0 copy-start.2
  7.2 0.0 copy-start.1
  7.2 0.0 copy-start.3
  7.2 0.0 all-gather.9.cloned.1.call-start
  7.3 6.5 %all-gather = bf16[32,3,8,128]{3,2,1,0:T(8,128)(2,1)} all-gather(bf16[16,3,8,128]{3,2,1,0:T(8,128)(2,1)} %param.9), channel_id=2, replica_groups=mesh['dom_0'=2,'dom_1'=8,'dom_2'=4,'orb'=4] {'dom_0'}, dimensions={0}, use_global_device_ids=true | all-gather | bytes 294912 | tf_op jit(solution)/shard_map/all_gather | solution.py:19
  13.7 0.0 all-gather.9.cloned.1.call-update
  13.8 0.0 all-gather.11.cloned.1.call-start
  13.8 39.6 %all-gather.9.cloned.1.call-done = bf16[16,16,3,8,128]{4,3,2,1,0:T(8,128)(2,1)} async-done(((bf16[2,16,3,8,128]{4,3,2,1,0:T(8,128)(2,1)}), bf16[16,16,3,8,128]{4,3,2,1,0:T(8,128)(2,1)}) %all-gather.9.cloned.1.call-update) | async-done | bytes 1572880 | tf_op jit(solution)/shard_map/all_gather | solution.py:19
  53.4 0.0 all-gather.11.cloned.1.call-update
  53.4 0.0 all-gather.7.cloned.1.call-start
  53.5 0.7 all-gather.7.cloned.1.call-update
  54.2 0.7 fusion.26
  54.8 0.8 fusion.17
  55.7 0.1 reshape.85
  55.8 0.8 gather_fusion
  56.5 0.1 reshape.101
  56.6 0.1 iota_compare_fusion.2
  56.7 0.1 fusion.23
  56.8 0.2 fusion.13
  57.0 68.7 %all-gather.11.cloned.1.call-done = bf16[32,2,16,3,8,128]{5,4,3,2,1,0:T(8,128)(2,1)} async-done(((bf16[8,2,16,3,8,128]{5,4,3,2,1,0:T(8,128)(2,1)}), bf16[32,2,16,3,8,128]{5,4,3,2,1,0:T(8,128)(2,1)}) %all-gather.11.cloned.1.call-update) | async-done | bytes 6291472 | tf_op jit(solution)/shard_map/all_gather | solution.py:19
  125.7 3.9 %copy.25 = bf16[2,8,4,16,3,8,128]{6,5,4,3,2,1,0:T(8,128)(2,1)S(1)} copy(bf16[2,8,4,16,3,8,128]{6,5,4,3,0,1,2:T(8,128)(2,1)} %bitcast.43) | data formatting | bytes 12582912 | tf_op jit(solution)/shard_map/transpose | solution.py:22
  129.6 4.9 %copy_bitcast_fusion = bf16[16,3,512,128]{3,2,1,0:T(8,128)(2,1)} fusion(bf16[2,8,4,16,3,8,128]{6,5,4,3,2,1,0:T(8,128)(2,1)S(1)} %copy.25), kind=kLoop, calls=%fused_computation.4 | loop fusion | bytes 12582912 | tf_op jit(solution)/shard_map/reshape | solution.py:13
  134.5 5.8 %gather_fusion.1 = bf16[32,512,128]{2,1,0:T(8,128)(2,1)} fusion(bf16[16,3,512,128]{3,2,1,0:T(8,128)(2,1)} %copy_bitcast_fusion, s32[32]{0:T(128)S(1)} %reshape.85), kind=kCustom, calls=%fused_computation.1 | custom fusion | bytes 8388864 | tf_op jit(solution)/shard_map/gather | solution.py:50
  140.3 54.4 %all-gather.7.cloned.1.call-done = bf16[2,4,1024,512]{3,2,1,0:T(8,128)(2,1)} async-done(((bf16[2,4,1024,128]{3,2,1,0:T(8,128)(2,1)}), bf16[2,4,1024,512]{3,2,1,0:T(8,128)(2,1)}) %all-gather.7.cloned.1.call-update) | async-done | bytes 8388624 | tf_op jit(solution)/shard_map/all_gather | solution.py:61
  194.7 9.8 %fusion.7 = bf16[2,4,1024,128]{2,3,1,0:T(8,128)(2,1)S(1)} fusion(bf16[2,4,1024,512]{3,2,1,0:T(8,128)(2,1)} %all-gather.7.cloned.1.call-done, bf16[2,4,4,512,128]{4,3,2,1,0:T(8,128)(2,1)} %bitcast.44, pred[2,4,4]{2,1,0:T(4,128)(4,1)S(1)} %fusion.23), kind=kOutput, calls=%fused_computation.11 | convolution fusion | flops 4298113024 | bytes 14680096 | tf_op jit(solution)/shard_map/glpi,glmij->gmpj/dot_general | solution.py:55
  204.6 2.5 %fusion.2 = f32[2,1,1024,1]{2,1,3,0:T(1,128)S(1)} fusion(f32[2,4,128,1]{2,3,1,0:T(1,128)S(1)} %bitcast.48, bf16[2,4,1024,128]{2,3,1,0:T(8,128)(2,1)S(1)} %fusion.7), kind=kOutput, calls=%fused_computation.6 | convolution fusion | flops 14680064 | bytes 2109440 | tf_op jit(solution)/shard_map/gmpj,gmj->gp/dot_general | solution.py:69
  207.1 0.6 broadcast_in_dim.15
  207.7 3.5 %all-to-all-start = ((f32[4,2,1024]{2,1,0:T(2,128)}), f32[4,2,1024]{2,1,0:T(2,128)S(1)}, u32[]{:S(2)}, u32[]{:S(2)}) async-start(f32[4,2,1024]{2,1,0:T(2,128)} %broadcast_in_dim.15), calls=%async_computation | async-start | bytes 65536 | tf_op jit(solution)/shard_map/all_to_all | solution.py:32
  211.2 2.5 %copy.29 = bf16[2,4,1024,128]{3,2,1,0:T(8,128)(2,1)} copy(bf16[2,4,1024,128]{2,3,1,0:T(8,128)(2,1)S(1)} %fusion.7) | data formatting | bytes 4194304
  213.7 2.1 all-to-all-done
  215.9 0.6 reduce_sum.9
  (6 shorter events, 0.0 us)
Async XLA Ops:
  7.2 49.6 %copy-start = (f32[16,128]{1,0:T(8,128)S(1)}, f32[16,128]{1,0:T(8,128)}, u32[]{:S(2)}) copy-start(f32[16,128]{1,0:T(8,128)} %param.11) | copy-start | bytes 24580
  7.2 49.5 %copy-start.2 = (s32[2,4]{1,0:T(2,128)S(1)}, s32[2,4]{1,0:T(2,128)}, u32[]{:S(2)}) copy-start(s32[2,4]{1,0:T(2,128)} %param.7) | copy-start | bytes 100
  7.2 48.6 %copy-start.1 = (s32[16,3]{0,1:T(4,128)S(1)}, s32[16,3]{0,1:T(4,128)}, u32[]{:S(2)}) copy-start(s32[16,3]{0,1:T(4,128)} %param.10) | copy-start | bytes 580
  7.2 49.4 %copy-start.3 = (s32[2]{0:T(128)S(1)}, s32[2]{0:T(128)}, u32[]{:S(2)}) copy-start(s32[2]{0:T(128)} %param.8) | copy-start | bytes 28
  7.2 46.2 %all-gather.9.cloned.1.call-start = ((), (), s32[]{:S(2)}) async-start(), calls=%async_computation.2 | async-start | bytes 1769472 | tf_op jit(solution)/shard_map/all_gather | solution.py:19
  13.8 111.9 %all-gather.11.cloned.1.call-start = ((), (), s32[]{:S(2)}) async-start(), calls=%async_computation.3 | async-start | bytes 7864320 | tf_op jit(solution)/shard_map/all_gather | solution.py:19
  53.4 141.3 %all-gather.7.cloned.1.call-start = ((), (), s32[]{:S(2)}) async-start(), calls=%async_computation.1 | async-start | bytes 10485760 | tf_op jit(solution)/shard_map/all_gather | solution.py:61
  207.7 8.2 %all-to-all-start = ((f32[4,2,1024]{2,1,0:T(2,128)}), f32[4,2,1024]{2,1,0:T(2,128)S(1)}, u32[]{:S(2)}, u32[]{:S(2)}) async-start(f32[4,2,1024]{2,1,0:T(2,128)} %broadcast_in_dim.15), calls=%async_computation | async-start | bytes 65536 | tf_op jit(solution)/shard_map/all_to_all | solution.py:32
Sparse Core Ops, SparseCore 0:
  13.9 39.4 all-gather.8
  55.2 70.4 all-gather.10
  127.5 67.1 all-gather.6
where the time goes:
time: 223 us
  waiting for transfers between devices  166 us (74%)
  local copies, waits for them, and re-layouts  18.7 us (8%)
  between operations  13.8 us (6%)
  matrix products  12.5 us (6%)
  blocking collectives  6.49 us (3%)
  starting transfers between devices  3.61 us (2%)
  other arithmetic  2.3 us (1%)
    all_gather x2, waiting for transfers between devices, all_blocks(): tiles = lax.all_gather(tiles, axes[k])  108 us
    all_gather x1, waiting for transfers between devices, local(): lax.all_gather(orbitals, 'orb', axis=3, tiled=True)  54.4 us
    dot_general x1, matrix products, rotate(): jnp.einsum('glpi,glmij->gmpj', values, tile_set, preferred_element_type=j...  9.84 us
    all_gather x1, blocking collectives, all_blocks(): tiles = lax.all_gather(tiles, axes[k])  6.49 us
    gather x1, local copies, waits for them, and re-layouts, select_tiles(): picked = band_full[source, column]  5.83 us
    reshape x1, local copies, waits for them, and re-layouts, laid_out(): return jnp.moveaxis(tiles, 0, dim).reshape(shape)  4.87 us
  transfers between devices with their start and end apart: 4, of which 4 were waited for; matrix products, arithmetic and copies ran while one was open for 9% of the time, Pallas kernels for 0%

commit v1 on v0

--- a/solution.py
+++ b/solution.py
@@ -5,6 +5,13 @@
 from jax.sharding import PartitionSpec as P
 
 DOM = ("dom_0", "dom_1", "dom_2")
+
+
+def exchange_gather(block, name, d):
+    size = lax.axis_size(name)
+    pieces = jnp.stack([block for _ in range(size)])
+    pieces = lax.all_to_all(pieces, name, split_axis=0, concat_axis=0)
+    return jnp.concatenate(pieces, axis=d)
 
 
 def laid_out(tiles, dim):
@@ -58,7 +65,7 @@
 def local(orbitals, slot_ids, slot_count, band_tiles, pattern, occupation):
     all_rows = whole_of(band_tiles, DOM, (0, 1, 2), 2)
     tile_set = select_tiles(all_rows, pattern, slot_ids, slot_count)
-    rotated_f = rotate(lax.all_gather(orbitals, "orb", axis=3, tiled=True), tile_set)
+    rotated_f = rotate(exchange_gather(orbitals, "orb", 3), tile_set)
     rotated = rotated_f.astype(jnp.bfloat16)
     onehot = (
         slot_ids[:, :, None] == jnp.arange(occupation.shape[0], dtype=jnp.int32)[None, None, :]

time: 223 us -> 234 us (1.049)
  local copies, waits for them, and re-layouts: 18.7 us -> 50.7 us
  waiting for transfers between devices: 166 us -> 134 us
  starting transfers between devices: 3.61 us -> 14.5 us
    all_to_all x0 -> x1, waiting for transfers between devices: none -> 92.3 us  [exchange_gather(): pieces = lax.all_to_all(pieces, name, split_axis=0, concat_axis=0)]
    all_gather x2, waiting for transfers between devices: 108 us -> 39.6 us  [all_blocks(): tiles = lax.all_gather(tiles, axes[k])]
    all_gather x1 -> x0, waiting for transfers between devices: 54.4 us -> none  [local(): lax.all_gather(orbitals, 'orb', axis=3, tiled=True)]
    reshape x0 -> x2, local copies, waits for them, and re-layouts: none -> 25.3 us  [exchange_gather(): return jnp.concatenate(pieces, axis=d)]
    all_to_all x0 -> x1, starting transfers between devices: none -> 10.2 us  [exchange_gather(): pieces = lax.all_to_all(pieces, name, split_axis=0, concat_axis=0)]
    another operation x0 -> x1, local copies, waits for them, and re-layouts: none -> 6.72 us  [exchange_gather(): pieces = jnp.stack([block for _ in range(size)])]
  transfers between devices with their start and end apart: 4 -> 4, of which waited for: 4 -> 3; matrix products, arithmetic and copies ran while one was open for 9% -> 15% of each run, Pallas kernels for 0% -> 0%
where the time goes in v1:
time: 234 us; the launch traced here: 233 us
  waiting for transfers between devices  134 us (57%)
  local copies, waits for them, and re-layouts  50.7 us (22%)
  starting transfers between devices  14.5 us (6%)
  between operations  14.1 us (6%)
  matrix products  12.5 us (5%)
  blocking collectives  6.49 us (3%)
    all_to_all x1, waiting for transfers between devices, exchange_gather(): pieces = lax.all_to_all(pieces, name, split_axis=0, concat_axis=0)  92.3 us
    all_gather x2, waiting for transfers between devices, all_blocks(): tiles = lax.all_gather(tiles, axes[k])  39.6 us
    reshape x2, local copies, waits for them, and re-layouts, exchange_gather(): return jnp.concatenate(pieces, axis=d)  25.3 us
    all_to_all x1, starting transfers between devices, exchange_gather(): pieces = lax.all_to_all(pieces, name, split_axis=0, concat_axis=0)  10.2 us
    dot_general x1, matrix products, rotate(): jnp.einsum('glpi,glmij->gmpj', values, tile_set, preferred_element_type=j...  9.84 us
    another operation x1, local copies, waits for them, and re-layouts, exchange_gather(): pieces = jnp.stack([block for _ in range(size)])  6.72 us
    all_gather x1, blocking collectives, all_blocks(): tiles = lax.all_gather(tiles, axes[k])  6.49 us
    gather x1, local copies, waits for them, and re-layouts, select_tiles(): picked = band_full[source, column]  5.83 us
  transfers between devices with their start and end apart: 4, of which 3 were waited for; matrix products, arithmetic and copies ran while one was open for 15% of the time, Pallas kernels for 0%

profile of v1, /device:TPU:1, one launch (start us, length us, event | category | flops | bytes accessed | tf_op | source)
XLA Modules:
  0.0 233.2 jit_solution(2059287385982845049)
XLA Ops:
  7.2 0.0 copy-start
  7.2 0.0 all-gather.6.cloned.1.call-start
  7.2 6.5 %all-gather = bf16[32,3,8,128]{3,2,1,0:T(8,128)(2,1)} all-gather(bf16[16,3,8,128]{3,2,1,0:T(8,128)(2,1)} %param.9), channel_id=2, replica_groups=mesh['dom_0'=2,'dom_1'=8,'dom_2'=4,'orb'=4] {'dom_0'}, dimensions={0}, use_global_device_ids=true | all-gather | bytes 294912 | tf_op jit(solution)/shard_map/all_gather | solution.py:26
  13.7 0.0 all-gather.6.cloned.1.call-update
  13.7 0.0 all-gather.8.cloned.1.call-start
  13.8 39.6 %all-gather.6.cloned.1.call-done = bf16[16,16,3,8,128]{4,3,2,1,0:T(8,128)(2,1)} async-done(((bf16[2,16,3,8,128]{4,3,2,1,0:T(8,128)(2,1)}), bf16[16,16,3,8,128]{4,3,2,1,0:T(8,128)(2,1)}) %all-gather.6.cloned.1.call-update) | async-done | bytes 1572880 | tf_op jit(solution)/shard_map/all_gather | solution.py:26
  53.4 0.0 all-gather.8.cloned.1.call-update
  53.4 6.7 %stack.2 = bf16[4,2,4,1024,128]{4,3,2,1,0:T(8,128)(2,1)} broadcast(bf16[2,4,1024,128]{3,2,1,0:T(8,128)(2,1)} %param.6), dimensions={1,2,3,4} | broadcast | bytes 10485760 | tf_op jit(solution)/shard_map/stack | solution.py:12
  60.1 10.2 %all-to-all-start = ((bf16[4,2,4,1024,128]{4,3,2,1,0:T(8,128)(2,1)}), bf16[4,2,4,1024,128]{4,3,2,1,0:T(8,128)(2,1)}, u32[]{:S(2)}, u32[]{:S(2)}) async-start(bf16[4,2,4,1024,128]{4,3,2,1,0:T(8,128)(2,1)} %stack.2), calls=%async_computation | async-start | bytes 16777216 | tf_op jit(solution)/shard_map/all_to_all | solution.py:13
  70.3 0.0 copy-done.2
  70.3 0.1 fusion.17
  70.4 0.1 reshape.95
  70.5 0.0 copy-done.1
  70.5 0.8 gather_fusion
  71.3 0.1 reshape.111
  71.4 0.0 copy-done.3
  71.4 0.1 iota_compare_fusion.2
  71.4 0.1 fusion.23
  71.5 0.2 fusion.13
  71.7 92.3 %all-to-all-done = bf16[4,2,4,1024,128]{4,3,2,1,0:T(8,128)(2,1)} async-done(((bf16[4,2,4,1024,128]{4,3,2,1,0:T(8,128)(2,1)}), bf16[4,2,4,1024,128]{4,3,2,1,0:T(8,128)(2,1)}, u32[]{:S(2)}, u32[]{:S(2)}) %all-to-all-start) | async-done | bytes 8388640 | tf_op jit(solution)/shard_map/all_to_all | solution.py:13
  164.1 12.2 %copy.29 = bf16[2,4,1024,4,128]{4,3,2,1,0:T(4,128)(2,1)} copy(bf16[2,4,1024,4,128]{4,2,1,0,3:T(8,128)(2,1)} %bitcast.8) | data formatting | bytes 16777216 | tf_op jit(solution)/shard_map/reshape | solution.py:14
  176.2 13.1 %reshape.112 = bf16[2,4,1024,512,1]{3,2,1,0,4:T(8,128)(2,1)} reshape(bf16[2,4,1024,4,128]{4,3,2,1,0:T(4,128)(2,1)} %copy.29) | data formatting | bytes 16777216 | tf_op jit(solution)/shard_map/reshape | solution.py:14
  189.4 3.9 %copy.27 = bf16[2,8,4,16,3,8,128]{6,5,4,3,2,1,0:T(8,128)(2,1)S(1)} copy(bf16[2,8,4,16,3,8,128]{6,5,4,3,0,1,2:T(8,128)(2,1)} %bitcast.42) | data formatting | bytes 12582912 | tf_op jit(solution)/shard_map/transpose | solution.py:29
  193.2 4.9 %copy_bitcast_fusion = bf16[16,3,512,128]{3,2,1,0:T(8,128)(2,1)} fusion(bf16[2,8,4,16,3,8,128]{6,5,4,3,2,1,0:T(8,128)(2,1)S(1)} %copy.27), kind=kLoop, calls=%fused_computation.4 | loop fusion | bytes 12582912 | tf_op jit(solution)/shard_map/reshape | solution.py:20
  198.1 5.8 %gather_fusion.1 = bf16[32,512,128]{2,1,0:T(8,128)(2,1)} fusion(bf16[16,3,512,128]{3,2,1,0:T(8,128)(2,1)} %copy_bitcast_fusion, s32[32]{0:T(128)S(1)} %reshape.95), kind=kCustom, calls=%fused_computation.1 | custom fusion | bytes 8388864 | tf_op jit(solution)/shard_map/gather | solution.py:57
  204.0 9.8 %fusion.7 = bf16[2,4,1024,128]{2,3,1,0:T(8,128)(2,1)S(1)} fusion(bf16[2,4,1024,512,1]{3,2,1,0,4:T(8,128)(2,1)} %reshape.112, bf16[2,4,4,512,128]{4,3,2,1,0:T(8,128)(2,1)} %bitcast.43, pred[2,4,4]{2,1,0:T(4,128)(4,1)S(1)} %fusion.23), kind=kOutput, calls=%fused_computation.11 | convolution fusion | flops 4298113024 | bytes 14680096 | tf_op jit(solution)/shard_map/glpi,glmij->gmpj/dot_general | solution.py:62
  213.8 2.5 %fusion.2 = f32[2,1,1024,1]{2,1,3,0:T(1,128)S(1)} fusion(f32[2,4,128,1]{2,3,1,0:T(1,128)S(1)} %bitcast.47, bf16[2,4,1024,128]{2,3,1,0:T(8,128)(2,1)S(1)} %fusion.7), kind=kOutput, calls=%fused_computation.6 | convolution fusion | flops 14680064 | bytes 2109440 | tf_op jit(solution)/shard_map/gmpj,gmj->gp/dot_general | solution.py:76
  216.3 0.6 broadcast_in_dim.15
  216.9 4.2 %all-to-all-start.1 = ((f32[4,2,1024]{2,1,0:T(2,128)}), f32[4,2,1024]{2,1,0:T(2,128)S(1)}, u32[]{:S(2)}, u32[]{:S(2)}) async-start(f32[4,2,1024]{2,1,0:T(2,128)} %broadcast_in_dim.15), calls=%async_computation.1 | async-start | bytes 65536 | tf_op jit(solution)/shard_map/all_to_all | solution.py:39
  221.1 2.5 %copy.32 = bf16[2,4,1024,128]{3,2,1,0:T(8,128)(2,1)} copy(bf16[2,4,1024,128]{2,3,1,0:T(8,128)(2,1)S(1)} %fusion.7) | data formatting | bytes 4194304
  223.6 2.1 all-to-all-done.1
  225.8 0.6 reduce_sum.9
  (8 shorter events, 0.0 us)
Async XLA Ops:
  7.2 64.4 %copy-start = (f32[16,128]{1,0:T(8,128)S(1)}, f32[16,128]{1,0:T(8,128)}, u32[]{:S(2)}) copy-start(f32[16,128]{1,0:T(8,128)} %param.11) | copy-start | bytes 24580
  7.2 46.2 %all-gather.6.cloned.1.call-start = ((), (), s32[]{:S(2)}) async-start(), calls=%async_computation.2 | async-start | bytes 1769472 | tf_op jit(solution)/shard_map/all_gather | solution.py:26
  13.7 175.6 %all-gather.8.cloned.1.call-start = ((), (), s32[]{:S(2)}) async-start(), calls=%async_computation.3 | async-start | bytes 7864320 | tf_op jit(solution)/shard_map/all_gather | solution.py:26
  60.1 10.2 %copy-start.2 = (s32[2,4]{1,0:T(2,128)S(1)}, s32[2,4]{1,0:T(2,128)}, u32[]{:S(2)}) copy-start(s32[2,4]{1,0:T(2,128)} %param.7) | copy-start | bytes 100
  60.1 10.4 %copy-start.1 = (s32[16,3]{0,1:T(4,128)S(1)}, s32[16,3]{0,1:T(4,128)}, u32[]{:S(2)}) copy-start(s32[16,3]{0,1:T(4,128)} %param.10) | copy-start | bytes 580
  60.1 103.9 %all-to-all-start = ((bf16[4,2,4,1024,128]{4,3,2,1,0:T(8,128)(2,1)}), bf16[4,2,4,1024,128]{4,3,2,1,0:T(8,128)(2,1)}, u32[]{:S(2)}, u32[]{:S(2)}) async-start(bf16[4,2,4,1024,128]{4,3,2,1,0:T(8,128)(2,1)} %stack.2), calls=%async_computation | async-start | bytes 16777216 | tf_op jit(solution)/shard_map/all_to_all | solution.py:13
  70.3 1.0 copy-start.3
  216.9 8.9 %all-to-all-start.1 = ((f32[4,2,1024]{2,1,0:T(2,128)}), f32[4,2,1024]{2,1,0:T(2,128)S(1)}, u32[]{:S(2)}, u32[]{:S(2)}) async-start(f32[4,2,1024]{2,1,0:T(2,128)} %broadcast_in_dim.15), calls=%async_computation.1 | async-start | bytes 65536 | tf_op jit(solution)/shard_map/all_to_all | solution.py:39
Sparse Core Ops, SparseCore 0:
  13.9 39.4 all-gather.5
  55.2 70.4 all-gather.7
